TPU v7x, 32 devices: a whole 2x2x4 slice. The times are simulated.
32 devices in a mesh: dp: 8 (over z, x), tensor: 4 (over y, core).
Axes of the slice: x: 2, y: 2, z: 4, core: 2. Of those that a mesh axis runs over, the one named last changes fastest.
Arguments:
- inputs: bfloat16 [2, 2048, 1280], P(None, 'dp'), may hold values from -6 to 6
- cotangent: bfloat16 [2, 2048, 1280], P(None, 'dp'), may hold values from -0.625 to 0.625
- w_in: bfloat16 [1280, 5120], P('dp', 'tensor'), may hold values from -0.15625 to 0.15625
- w_out: bfloat16 [1280, 5120], P('dp', 'tensor'), may hold values from -0.078125 to 0.078125
- grad_in: float32 [1280, 5120], P('dp', 'tensor'), may hold values from -24 to 24
- grad_out: float32 [1280, 5120], P('dp', 'tensor'), may hold values from -24 to 24
Outputs:
- branch_output: bfloat16 [2, 2048, 1280], P(None, 'dp', 'tensor')
- ascent_in: float32 [1280, 5120], P('dp', 'tensor')
- ascent_out: float32 [1280, 5120], P('dp', 'tensor')
- new_grad_in: float32 [1280, 5120], P('dp', 'tensor')
- new_grad_out: float32 [1280, 5120], P('dp', 'tensor')
All inputs are finite; a program needn't handle non-finite values.
Results may differ from a plain program's by a relative error of at most 0.0064.
Values may be sent and summed in bfloat16 or wider, within the bound.
A program may use at most 128 MiB of HBM per device.

v0:
```python
import math
import jax
import jax.numpy as jnp
from jax import lax
from jax.sharding import PartitionSpec as P

D = 1280
FF = 5120
RHO = 0.1
ETA = 0.01


def gelu_parts(pre):
    cdf = 0.5 * (1.0 + lax.erf(pre * 0.7071067811865476))
    dens = jnp.exp(-0.5 * pre * pre) * 0.3989422804014327
    return (pre * cdf, cdf + pre * dens)


def token_product(left, right):
    return lax.dot_general(
        left, right, (((0,), (0,)), ((), ())), preferred_element_type=jnp.float32
    )


def local(inputs, cotangent, w_in, w_out, grad_in, grad_out):
    scale_in = jnp.abs(w_in.astype(jnp.float32)) + ETA
    scale_out = jnp.abs(w_out.astype(jnp.float32)) + ETA
    scaled_in = scale_in * grad_in
    scaled_out = scale_out * grad_out
    partial_sq = jnp.sum(scaled_in * scaled_in) + jnp.sum(scaled_out * scaled_out)
    row_total = lax.psum(partial_sq, "tensor")
    total = lax.psum(row_total, "dp")
    factor = math.sqrt(2.0 * D * FF) / jnp.sqrt(total + 1.0)
    ascent_in = factor * scaled_in
    ascent_out = factor * scaled_out
    moved_in = (w_in.astype(jnp.float32) + RHO * scale_in * ascent_in).astype(jnp.bfloat16)
    moved_out = (w_out.astype(jnp.float32) + RHO * scale_out * ascent_out).astype(jnp.bfloat16)
    micro = inputs.shape[0]
    full_in, full_out = (
        lax.all_gather(moved_in, "dp", axis=0, tiled=True),
        lax.all_gather(moved_out, "dp", axis=0, tiled=True),
    )
    outputs = []
    acts = []
    deltas = []
    for index in range(micro):
        rows = inputs[index]
        grads_y = cotangent[index]
        pre = jnp.dot(rows, full_in, preferred_element_type=jnp.float32)
        act, slope = gelu_parts(pre)
        act = act.astype(jnp.bfloat16)
        partial_y = lax.dot_general(
            act, full_out, (((1,), (1,)), ((), ())), preferred_element_type=jnp.float32
        )
        shared_y = lax.psum_scatter(partial_y, "tensor", scatter_dimension=1, tiled=True)
        outputs.append(shared_y.astype(jnp.bfloat16))
        back = jnp.dot(grads_y, full_out, preferred_element_type=jnp.float32)
        acts.append(act)
        deltas.append((back * slope).astype(jnp.bfloat16))
    branch_output = jnp.stack(outputs)
    flat_x = inputs.reshape(-1, inputs.shape[2])
    flat_dy = cotangent.reshape(-1, cotangent.shape[2])
    flat_delta = jnp.concatenate(deltas, axis=0)
    flat_act = jnp.concatenate(acts, axis=0)
    whole_in = token_product(flat_x, flat_delta)
    whole_out = token_product(flat_dy, flat_act)
    new_in, new_out = (
        lax.psum_scatter(whole_in, "dp", scatter_dimension=0, tiled=True),
        lax.psum_scatter(whole_out, "dp", scatter_dimension=0, tiled=True),
    )
    return (branch_output, ascent_in, ascent_out, new_in, new_out)


def solution(mesh):
    return jax.shard_map(
        local,
        mesh=mesh,
        in_specs=(
            P(None, "dp", None),
            P(None, "dp", None),
            P("dp", "tensor"),
            P("dp", "tensor"),
            P("dp", "tensor"),
            P("dp", "tensor"),
        ),
        out_specs=(
            P(None, "dp", "tensor"),
            P("dp", "tensor"),
            P("dp", "tensor"),
            P("dp", "tensor"),
            P("dp", "tensor"),
        ),
        check_vma=False,
    )
```

profile of v0, /device:TPU:0, one launch (start us, length us, event | category | flops | bytes accessed | tf_op | source)
XLA Modules:
  0.0 481.0 jit_solution(9765077952277714172)
XLA Ops:
  7.2 0.0 copy-start
  7.2 0.0 copy-start.2
  7.2 0.0 all-gather.3.cloned.1.call-start
  7.2 2.6 multiply_reduce_fusion
  11.2 8.9 %psum.14 = f32[]{:T(128)} all-reduce(f32[]{:T(128)S(6)} %add.44), channel_id=1, replica_groups=mesh['dp'=8,'tensor'=4] {'tensor'}, use_global_device_ids=true, to_apply=%region_2.0 | all-reduce | flops 1 | bytes 8 | tf_op jit(solution)/shard_map/psum | solution.py:31
  20.1 22.3 %psum.15 = f32[]{:T(128)} all-reduce(f32[]{:T(128)} %psum.14), channel_id=1, replica_groups=mesh['dp'=8,'tensor'=4] {'dp'}, use_global_device_ids=true, to_apply=%region_3.0 | all-reduce | flops 1 | bytes 8 | tf_op jit(solution)/shard_map/psum | solution.py:32
  43.0 0.0 copy-start.1
  43.1 0.0 copy-start.3
  43.1 1.2 fusion.22
  44.3 0.0 all-gather.3.cloned.1.call-update
  44.3 0.0 all-gather.5.cloned.1.call-start
  44.4 0.2 copy-done.3
  44.6 1.2 fusion.27
  45.8 0.0 all-gather.5.cloned.1.call-update
  45.8 0.0 reduce-scatter.11.cloned.1.call-start
  45.9 56.3 %all-gather.3.cloned.1.call-done = bf16[1280,1280]{1,0:T(8,128)(2,1)} async-done(((bf16[160,1280]{1,0:T(8,128)(2,1)}), bf16[1280,1280]{1,0:T(8,128)(2,1)}) %all-gather.3.cloned.1.call-update) | async-done | bytes 3276816 | tf_op jit(solution)/shard_map/all_gather | solution.py:40
  102.2 4.2 multiply_convert_fusion
  106.4 58.7 %all-gather.5.cloned.1.call-done = bf16[1280,1280]{1,0:T(8,128)(2,1)} async-done(((bf16[160,1280]{1,0:T(8,128)(2,1)}), bf16[1280,1280]{1,0:T(8,128)(2,1)}) %all-gather.5.cloned.1.call-update) | async-done | bytes 3276816 | tf_op jit(solution)/shard_map/all_gather | solution.py:41
  165.1 4.1 fusion.43
  169.2 0.0 copy-done.7
  169.2 0.0 reduce-scatter.11.cloned.1.call-update
  169.2 0.0 reduce-scatter.9.cloned.1.call-start
  169.2 4.4 multiply_convert_fusion.1
  173.6 0.8 copy-done.8
  174.5 2.1 fusion.42
  176.6 0.0 reduce-scatter.9.cloned.1.call-update
  176.6 0.0 reduce-scatter.15.cloned.1.call-start
  176.7 6.4 %convolution_bitcast_fusion = f32[1280,1280]{0,1:T(8,128)} fusion(bf16[512,1280]{1,0:T(8,128)(2,1)} %bitcast.54, bf16[256,1280]{1,0:T(8,128)(2,1)} %copy-done.7, bf16[256,1280]{1,0:T(8,128)(2,1)} %copy-done.8), kind=kOutput, calls=%fused_computation | convolution fusion | flops 1680343040 | bytes 9175040 | tf_op jit(solution)/shard_map/dot_general | solution.py:20
  183.0 8.2 %copy.17 = f32[1280,1280]{1,0:T(8,128)} copy(f32[1280,1280]{0,1:T(8,128)} %convolution_bitcast_fusion) | data formatting | bytes 13107200
  191.3 0.0 reduce-scatter.15.cloned.1.call-update
  191.3 0.0 reduce-scatter.13.cloned.1.call-start
  191.3 0.0 copy-start.5
  191.4 0.0 copy-start.9
  191.4 2.8 fusion.3
  194.2 0.0 copy-done.5
  194.2 0.0 copy-start.6
  194.2 1.1 fusion.2
  195.3 0.2 copy-done.6
  195.5 4.6 convolution_bitcast_fusion.1
  200.1 8.3 %copy.15 = f32[1280,1280]{1,0:T(8,128)} copy(f32[1280,1280]{0,1:T(8,128)} %convolution_bitcast_fusion.1) | data formatting | bytes 13107200
  208.4 0.0 reduce-scatter.13.cloned.1.call-update
  208.4 0.0 reduce-scatter.11.cloned.1.call-done
  208.4 1.0 convert_bitcast_fusion
  209.4 13.9 %reduce-scatter.9.cloned.1.call-done = f32[256,320]{0,1:T(8,128)} async-done(((f32[256,1280]{0,1:T(8,128)}), f32[256,320]{0,1:T(8,128)}) %reduce-scatter.9.cloned.1.call-update) | async-done | bytes 327696 | tf_op jit(solution)/shard_map/reduce_scatter | solution.py:55
  223.3 1.0 convert_bitcast_fusion.1
  224.3 0.8 pad_maximum_fusion
  225.0 124.1 %reduce-scatter.15.cloned.1.call-done = f32[160,1280]{1,0:T(8,128)} async-done(((f32[1280,1280]{1,0:T(8,128)}), f32[160,1280]{1,0:T(8,128)}) %reduce-scatter.15.cloned.1.call-update) | async-done | bytes 819216
  349.1 125.1 %reduce-scatter.13.cloned.1.call-done = f32[160,1280]{1,0:T(8,128)} async-done(((f32[1280,1280]{1,0:T(8,128)}), f32[160,1280]{1,0:T(8,128)}) %reduce-scatter.13.cloned.1.call-update) | async-done | bytes 819216
  (8 shorter events, 0.0 us)
Async XLA Ops:
  7.2 35.9 %copy-start = (f32[160,1280]{1,0:T(8,128)S(1)}, f32[160,1280]{1,0:T(8,128)}, u32[]{:S(2)}) copy-start(f32[160,1280]{1,0:T(8,128)} %param.10) | copy-start | bytes 2457604
  7.2 35.9 %copy-start.2 = (bf16[160,1280]{1,0:T(8,128)(2,1)S(1)}, bf16[160,1280]{1,0:T(8,128)(2,1)}, u32[]{:S(2)}) copy-start(bf16[160,1280]{1,0:T(8,128)(2,1)} %param.8) | copy-start | bytes 1228804
  7.2 95.0 %all-gather.3.cloned.1.call-start = ((), (), s32[]{:S(2)}) async-start(), calls=%async_computation.4 | async-start | bytes 3686400 | tf_op jit(solution)/shard_map/all_gather | solution.py:40
  43.0 1.4 copy-start.1
  43.1 1.5 copy-start.3
  44.3 120.8 %all-gather.5.cloned.1.call-start = ((), (), s32[]{:S(2)}) async-start(), calls=%async_computation.5 | async-start | bytes 3686400 | tf_op jit(solution)/shard_map/all_gather | solution.py:41
  45.8 162.6 %reduce-scatter.11.cloned.1.call-start = ((), (), s32[]{:S(2)}) async-start(), calls=%async_computation.7 | async-start | bytes 1638400 | tf_op jit(solution)/shard_map/reduce_scatter | solution.py:55
  106.4 62.8 %copy-start.7 = (bf16[256,1280]{1,0:T(8,128)(2,1)}, bf16[256,1280]{1,0:T(8,128)(2,1)S(1)}, u32[]{:S(2)}) copy-start(bf16[256,1280]{1,0:T(8,128)(2,1)S(1)} %get-tuple-element.19) | copy-start | bytes 1966084
  169.2 5.3 %copy-start.4 = (bf16[1280,1280]{1,0:T(8,128)(2,1)S(1)}, bf16[1280,1280]{1,0:T(8,128)(2,1)}, u32[]{:S(2)}) copy-start(bf16[1280,1280]{1,0:T(8,128)(2,1)} %all-gather.5.cloned.1.call-done) | copy-start | bytes 9830404
  169.2 54.1 %reduce-scatter.9.cloned.1.call-start = ((), (), s32[]{:S(2)}) async-start(), calls=%async_computation.6 | async-start | bytes 1638400 | tf_op jit(solution)/shard_map/reduce_scatter | solution.py:55
  173.6 0.8 copy-start.8
  176.6 172.5 %reduce-scatter.15.cloned.1.call-start = ((), (), s32[]{:S(2)}) async-start(), calls=%async_computation.9 | async-start | bytes 7372800
  191.3 282.8 %reduce-scatter.13.cloned.1.call-start = ((), (), s32[]{:S(2)}) async-start(), calls=%async_computation.8 | async-start | bytes 7372800
  191.3 2.8 copy-start.5
  191.4 2.8 copy-start.9
  194.2 1.3 copy-start.6
Sparse Core Ops, SparseCore 0:
  44.5 57.6 all-gather.2
  104.9 60.1 all-gather.4
  169.3 25.0 reduce-scatter.10
  196.8 26.3 reduce-scatter.8
  227.3 121.7 reduce-scatter.14
  353.1 120.9 reduce-scatter.12
where the time goes:
time: 482 us; the launch traced here: 481 us
  waiting for transfers between devices  378 us (78%)
  blocking collectives  31.2 us (6%)
  matrix products  29.7 us (6%)
  local copies, waits for them, and re-layouts  17.7 us (4%)
  between operations  16.2 us (3%)
  other arithmetic  7.87 us (2%)
    unnamed x8, waiting for transfers between devices  249 us
    all_gather x1, waiting for transfers between devices, local(): lax.all_gather(moved_out, 'dp', axis=0, tiled=True)  58.7 us
    all_gather x1, waiting for transfers between devices, local(): lax.all_gather(moved_in, 'dp', axis=0, tiled=True)  56.3 us
    psum x1, blocking collectives, local(): total = lax.psum(row_total, 'dp')  22.3 us
    unnamed x22, local copies, waits for them, and re-layouts  17.7 us
    reduce_scatter x2, waiting for transfers between devices, local(): lax.psum_scatter(partial_y, 'tensor', scatter_dimension=1, tiled=True)  13.9 us
    dot_general x2, matrix products, token_product(): lax.dot_general(left, right, (((0,), (0,)), ((), ())), preferred_element_...  11 us
  transfers between devices with their start and end apart: 6, of which 5 were waited for; matrix products, arithmetic and copies ran while one was open for 10% of the time, Pallas kernels for 0%

commit v1 on v0

--- a/solution.py
+++ b/solution.py
@@ -8,6 +8,27 @@
 FF = 5120
 RHO = 0.1
 ETA = 0.01
+
+
+def in_order(pieces, dim):
+    dims = list(pieces.shape[1:])
+    dims[dim] *= pieces.shape[0]
+    return jnp.moveaxis(pieces, 0, dim).reshape(dims)
+
+
+def collected_by_bits(array, axis):
+    size, index = (lax.axis_size(axis), lax.axis_index(axis))
+    blocks, distance = (array[None], 1)
+    while distance < size:
+        other = lax.ppermute(blocks, axis, [(i, i ^ distance) for i in range(size)])
+        low = index & distance == 0
+        blocks = jnp.concatenate([jnp.where(low, blocks, other), jnp.where(low, other, blocks)])
+        distance *= 2
+    return blocks
+
+
+def doubled_up(x, axis, dim):
+    return in_order(collected_by_bits(x, axis), dim)
 
 
 def gelu_parts(pre):
@@ -38,7 +59,7 @@
     micro = inputs.shape[0]
     full_in, full_out = (
         lax.all_gather(moved_in, "dp", axis=0, tiled=True),
-        lax.all_gather(moved_out, "dp", axis=0, tiled=True),
+        doubled_up(moved_out, "dp", 0),
     )
     outputs = []
     acts = []

time: 482 us -> 498 us (1.033)
  waiting for transfers between devices: 378 us -> 393 us
    ppermute x0 -> x3, waiting for transfers between devices: none -> 130 us  [collected_by_bits(): other = lax.ppermute(blocks, axis, [(i, i ^ distance) for i in range(size)])]
    all_gather x1 -> x0, waiting for transfers between devices: 58.7 us -> none  [local(): lax.all_gather(moved_out, 'dp', axis=0, tiled=True)]
    all_gather x1, waiting for transfers between devices: 56.3 us -> 0.02 us  [local(): lax.all_gather(moved_in, 'dp', axis=0, tiled=True)]
    unnamed x22 -> x20, local copies, waits for them, and re-layouts: 17.7 us -> 18.6 us
    unnamed x8 -> x7, waiting for transfers between devices: 249 us -> 249 us
  transfers between devices with their start and end apart: 6 -> 8, of which waited for: 5 -> 6; matrix products, arithmetic and copies ran while one was open for 10% -> 9% of each run, Pallas kernels for 0% -> 0%
where the time goes in v1:
time: 498 us; the launch traced here: 497 us
  waiting for transfers between devices  393 us (79%)
  blocking collectives  31.2 us (6%)
  matrix products  27.6 us (6%)
  local copies, waits for them, and re-layouts  18.6 us (4%)
  between operations  16 us (3%)
  other arithmetic  10.1 us (2%)
    unnamed x7, waiting for transfers between devices  249 us
    ppermute x3, waiting for transfers between devices, collected_by_bits(): other = lax.ppermute(blocks, axis, [(i, i ^ distance) for i in range(size)])  130 us
    psum x1, blocking collectives, local(): total = lax.psum(row_total, 'dp')  22.3 us
    unnamed x20, local copies, waits for them, and re-layouts  18.6 us
    reduce_scatter x2, waiting for transfers between devices, local(): lax.psum_scatter(partial_y, 'tensor', scatter_dimension=1, tiled=True)  13.7 us
    dot_general x2, matrix products, token_product(): lax.dot_general(left, right, (((0,), (0,)), ((), ())), preferred_element_...  11 us
  transfers between devices with their start and end apart: 8, of which 6 were waited for; matrix products, arithmetic and copies ran while one was open for 9% of the time, Pallas kernels for 0%

profile of v1, /device:TPU:0, one launch (start us, length us, event | category | flops | bytes accessed | tf_op | source)
XLA Modules:
  0.0 497.0 jit_solution(6864161073116264421)
XLA Ops:
  7.2 0.0 all-gather.2.cloned.1.call-start
  7.2 2.6 multiply_reduce_fusion
  11.2 8.9 %psum.14 = f32[]{:T(128)} all-reduce(f32[]{:T(128)S(6)} %add.44), channel_id=1, replica_groups=mesh['dp'=8,'tensor'=4] {'tensor'}, use_global_device_ids=true, to_apply=%region_2.0 | all-reduce | flops 1 | bytes 8 | tf_op jit(solution)/shard_map/psum | solution.py:52
  20.1 22.3 %psum.15 = f32[]{:T(128)} all-reduce(f32[]{:T(128)} %psum.14), channel_id=1, replica_groups=mesh['dp'=8,'tensor'=4] {'dp'}, use_global_device_ids=true, to_apply=%region_3.0 | all-reduce | flops 1 | bytes 8 | tf_op jit(solution)/shard_map/psum | solution.py:53
  43.1 1.2 fusion.22
  44.3 0.0 all-gather.2.cloned.1.call-update
  44.3 0.0 reduce-scatter.11.cloned.1.call-start
  44.4 0.2 copy-done.3
  44.6 1.1 fusion.38
  45.7 12.2 %collective-permute-done = bf16[1,160,1280]{2,1,0:T(8,128)(2,1)S(1)} collective-permute-done((bf16[1,160,1280]{2,1,0:T(8,128)(2,1)S(1)}, bf16[1,160,1280]{2,1,0:T(8,128)(2,1)S(1)}, u32[]{:S(2)}, u32[]{:S(2)}) %collective-permute-start) | collective-permute-done | bytes 409632 | tf_op jit(solution)/shard_map/ppermute | solution.py:23
  57.9 0.1 broadcast_select_fusion.5
  57.9 0.1 pad_maximum_fusion.2
  58.0 0.1 collective-permute-start.1
  58.1 22.8 %collective-permute-done.1 = bf16[2,160,1280]{2,1,0:T(8,128)(2,1)S(1)} collective-permute-done((bf16[2,160,1280]{2,1,0:T(8,128)(2,1)S(1)}, bf16[2,160,1280]{2,1,0:T(8,128)(2,1)S(1)}, u32[]{:S(2)}, u32[]{:S(2)}) %collective-permute-start.1) | collective-permute-done | bytes 819232 | tf_op jit(solution)/shard_map/ppermute | solution.py:23
  80.9 0.1 broadcast_select_fusion.3
  81.0 0.1 pad_maximum_fusion.1
  81.2 0.1 collective-permute-start.2
  81.3 95.1 %collective-permute-done.2 = bf16[4,160,1280]{2,1,0:T(8,128)(2,1)} collective-permute-done((bf16[4,160,1280]{2,1,0:T(8,128)(2,1)S(1)}, bf16[4,160,1280]{2,1,0:T(8,128)(2,1)}, u32[]{:S(2)}, u32[]{:S(2)}) %collective-permute-start.2) | collective-permute-done | bytes 1638432 | tf_op jit(solution)/shard_map/ppermute | solution.py:23
  176.4 1.6 broadcast_select_fusion.1
  178.0 0.3 pad_maximum_fusion
  178.3 0.0 all-gather.2.cloned.1.call-done
  178.3 4.2 multiply_convert_fusion
  182.6 0.8 copy-done.6
  183.4 2.1 fusion.44
  185.5 0.0 reduce-scatter.11.cloned.1.call-update
  185.6 0.0 reduce-scatter.9.cloned.1.call-start
  185.6 4.2 multiply_convert_fusion.1
  189.8 0.8 copy-done.7
  190.7 2.1 fusion.43
  192.8 0.0 reduce-scatter.9.cloned.1.call-update
  192.8 0.0 reduce-scatter.15.cloned.1.call-start
  192.9 6.4 %convolution_bitcast_fusion = f32[1280,1280]{0,1:T(8,128)} fusion(bf16[512,1280]{1,0:T(8,128)(2,1)} %bitcast.61, bf16[256,1280]{1,0:T(8,128)(2,1)} %copy-done.6, bf16[256,1280]{1,0:T(8,128)(2,1)} %copy-done.7), kind=kOutput, calls=%fused_computation | convolution fusion | flops 1680343040 | bytes 9175040 | tf_op jit(solution)/shard_map/dot_general | solution.py:41
  199.2 8.3 %copy.17 = f32[1280,1280]{1,0:T(8,128)} copy(f32[1280,1280]{0,1:T(8,128)} %convolution_bitcast_fusion) | data formatting | bytes 13107200
  207.5 0.0 reduce-scatter.15.cloned.1.call-update
  207.5 0.2 reduce-scatter.13.cloned.1.call-start
  207.8 2.8 fusion.3
  210.6 1.1 fusion.2
  211.8 0.2 copy-done.5
  211.9 4.6 convolution_bitcast_fusion.1
  216.5 8.3 %copy.15 = f32[1280,1280]{1,0:T(8,128)} copy(f32[1280,1280]{0,1:T(8,128)} %convolution_bitcast_fusion.1) | data formatting | bytes 13107200
  224.8 0.0 reduce-scatter.13.cloned.1.call-update
  224.8 0.0 reduce-scatter.11.cloned.1.call-done
  224.9 1.0 convert_bitcast_fusion
  225.9 13.6 %reduce-scatter.9.cloned.1.call-done = f32[256,320]{0,1:T(8,128)} async-done(((f32[256,1280]{0,1:T(8,128)}), f32[256,320]{0,1:T(8,128)}) %reduce-scatter.9.cloned.1.call-update) | async-done | bytes 327696 | tf_op jit(solution)/shard_map/reduce_scatter | solution.py:76
  239.5 1.0 convert_bitcast_fusion.1
  240.5 0.8 pad_maximum_fusion.3
  241.3 124.1 %reduce-scatter.15.cloned.1.call-done = f32[160,1280]{1,0:T(8,128)} async-done(((f32[1280,1280]{1,0:T(8,128)}), f32[160,1280]{1,0:T(8,128)}) %reduce-scatter.15.cloned.1.call-update) | async-done | bytes 819216
  365.4 125.1 %reduce-scatter.13.cloned.1.call-done = f32[160,1280]{1,0:T(8,128)} async-done(((f32[1280,1280]{1,0:T(8,128)}), f32[160,1280]{1,0:T(8,128)}) %reduce-scatter.13.cloned.1.call-update) | async-done | bytes 819216
  (15 shorter events, 0.0 us)
Async XLA Ops:
  7.2 35.9 %copy-start = (f32[160,1280]{1,0:T(8,128)S(1)}, f32[160,1280]{1,0:T(8,128)}, u32[]{:S(2)}) copy-start(f32[160,1280]{1,0:T(8,128)} %param.10) | copy-start | bytes 2457604
  7.2 35.9 %copy-start.2 = (bf16[160,1280]{1,0:T(8,128)(2,1)S(1)}, bf16[160,1280]{1,0:T(8,128)(2,1)}, u32[]{:S(2)}) copy-start(bf16[160,1280]{1,0:T(8,128)(2,1)} %param.8) | copy-start | bytes 1228804
  7.2 171.1 %all-gather.2.cloned.1.call-start = ((), (), s32[]{:S(2)}) async-start(), calls=%async_computation.4 | async-start | bytes 3686400 | tf_op jit(solution)/shard_map/all_gather | solution.py:61
  43.0 1.4 copy-start.1
  43.1 1.5 copy-start.3
  44.3 180.5 %reduce-scatter.11.cloned.1.call-start = ((), (), s32[]{:S(2)}) async-start(), calls=%async_computation.6 | async-start | bytes 1638400 | tf_op jit(solution)/shard_map/reduce_scatter | solution.py:76
  45.7 12.2 %collective-permute-start = (bf16[1,160,1280]{2,1,0:T(8,128)(2,1)S(1)}, bf16[1,160,1280]{2,1,0:T(8,128)(2,1)S(1)}, u32[]{:S(2)}, u32[]{:S(2)}) collective-permute-start(bf16[1,160,1280]{2,1,0:T(8,128)(2,1)S(1)} %get-tuple-element.15), channel_id=1, source_target_pairs={{0,4},{4,0},{8,12},{12,8},{16,20},{20,16},{24,28},{28,24},{1,5},{5... | collective-permute-start | bytes 1228808 | tf_op jit(solution)/shard_map/ppermute | solution.py:23
  58.0 22.9 %collective-permute-start.1 = (bf16[2,160,1280]{2,1,0:T(8,128)(2,1)S(1)}, bf16[2,160,1280]{2,1,0:T(8,128)(2,1)S(1)}, u32[]{:S(2)}, u32[]{:S(2)}) collective-permute-start(bf16[2,160,1280]{2,1,0:T(8,128)(2,1)S(1)} %pad_maximum_fusion.2), channel_id=1, source_target_pairs={{0,8},{4,12},{8,0},{12,4},{16,24},{20,28},{24,16},{28,20},{1,9},{5... | collective-permute-start | bytes 2457608 | tf_op jit(solution)/shard_map/ppermute | solution.py:23
  81.2 95.2 %collective-permute-start.2 = (bf16[4,160,1280]{2,1,0:T(8,128)(2,1)S(1)}, bf16[4,160,1280]{2,1,0:T(8,128)(2,1)}, u32[]{:S(2)}, u32[]{:S(2)}) collective-permute-start(bf16[4,160,1280]{2,1,0:T(8,128)(2,1)S(1)} %pad_maximum_fusion.1), channel_id=1, source_target_pairs={{0,16},{4,20},{8,24},{12,28},{16,0},{20,4},{24,8},{28,12},{1,17},{... | collective-permute-start | bytes 4915208 | tf_op jit(solution)/shard_map/ppermute | solution.py:23
  182.6 0.8 copy-start.6
  185.6 54.0 %reduce-scatter.9.cloned.1.call-start = ((), (), s32[]{:S(2)}) async-start(), calls=%async_computation.5 | async-start | bytes 1638400 | tf_op jit(solution)/shard_map/reduce_scatter | solution.py:76
  189.8 0.8 copy-start.7
  192.8 172.6 %reduce-scatter.15.cloned.1.call-start = ((), (), s32[]{:S(2)}) async-start(), calls=%async_computation.8 | async-start | bytes 7372800
  207.5 282.9 %reduce-scatter.13.cloned.1.call-start = ((), (), s32[]{:S(2)}) async-start(), calls=%async_computation.7 | async-start | bytes 7372800
  207.8 2.8 copy-start.4
  207.8 2.8 copy-start.8
  210.6 1.3 copy-start.5
Sparse Core Ops, SparseCore 0:
  44.5 110.3 all-gather.1
  185.7 24.7 reduce-scatter.10
  213.0 26.4 reduce-scatter.8
  243.6 121.7 reduce-scatter.14
  369.4 120.9 reduce-scatter.12
